TPU v7x, 32 devices: a whole 2x2x4 slice. The times are simulated.
32 devices in a mesh: gz: 8 (over z, y), xy: 4 (over x, core).
Axes of the slice: x: 2, y: 2, z: 4, core: 2. Of those that a mesh axis runs over, the one named last changes fastest.
Arguments:
- image: float32 [64, 512, 512], P('gz', 'xy'), may hold values from -6 to 6
- offsets: int32 [4, 64, 4, 4], P(None, 'gz', 'xy'), may hold values from -6 to 6
- frac_index: int32 [4, 64, 4, 4], P(None, 'gz', 'xy'), may hold values from 0 to 15
- fractions: float32 [16, 3], replicated, may hold values from 0 to 1
Outputs:
- transported: float32 [64, 512, 512], P('gz', 'xy')
All inputs are finite; a program needn't handle non-finite values.
Results may differ from a plain program's by a relative error of at most 0.0003.
Values sent between devices are 32-bit elements; how exact they have to be, the bound alone decides.
A program may use at most 128 MiB of HBM per device.

v0:
```python
import functools

import jax
import jax.numpy as jnp
from jax import lax
from jax.experimental import pallas as pl
from jax.experimental.pallas import tpu as pltpu
from jax.sharding import PartitionSpec as P

MESH = pl.DeviceIdType.MESH
LANES = 128


def slot_of(g, n, strip):
    if n % 2 == 0:
        far, near = g // 2, g % 2
        g = far + near * (n - 1 - 2 * far)
    return g + (strip % 2) * (n - 1 - 2 * g)


def device_at(slot, n, strip):
    slot = slot + (strip % 2) * (n - 1 - 2 * slot)
    if n % 2:
        return slot
    half = slot // (n // 2)
    return 2 * (slot + half * (n - 1 - 2 * slot)) + half


def fused_kernel(
    n, n_xy, steps,
    image_ref, meta_ref, table_ref, out_ref, meta_all_ref,
    landed, cells_a, cells_b, final, send_high, send_low, recv_high, recv_low, meta_s,
    in_send, in_recv, meta_send, meta_recv, halo_send, halo_recv, out_send, out_recv, local_sem,
):
    planes = image_ref.shape[0]
    nz = n * planes
    rows = final.shape[1]
    blocks = final.shape[2] // LANES
    pair = 2 if n_xy % 2 == 0 else 1
    pieces = n * pair
    me = lax.axis_index("gz")
    xy = lax.axis_index("xy")
    strip, half = xy // pair, lax.rem(xy, pair)
    piece = slot_of(me, n, strip) * pair + half
    home = strip * pair + piece // n
    part = lax.rem(piece, n)
    is_home = home == xy

    def holder(line):
        strip_at, piece_at = line // pieces, lax.rem(line, pieces)
        return (
            device_at(piece_at // pair, n, strip_at),
            strip_at * pair + lax.rem(piece_at, pair),
        )

    line = strip * pieces + piece
    next_id = holder(lax.rem(line + 1, n * n_xy))
    prev_id = holder(lax.rem(line + n * n_xy - 1, n * n_xy))

    barrier = pltpu.get_barrier_semaphore()
    for i in range(1, pieces):
        other = lax.rem(half * n + me + i, pieces)
        pl.semaphore_signal(
            barrier, inc=1, device_id=(lax.rem(other, n), strip * pair + other // n), device_id_type=MESH)
    for neighbour in (next_id, prev_id):
        pl.semaphore_signal(barrier, inc=1, device_id=neighbour, device_id_type=MESH)
    pl.semaphore_wait(barrier, pieces + 1)

    def share(i):
        return pl.ds(pl.multiple_of(i * rows, 8), rows)

    def slab(g):
        return pl.ds(g * planes, planes)

    def eight(g):
        return pl.ds(pl.multiple_of(g * 8, 8), 8)

    def taker(i):
        return holder(strip * pieces + half * n + i)

    def meta_copy(i):
        return pltpu.make_async_remote_copy(
            src_ref=meta_ref, dst_ref=meta_all_ref.at[eight(me)],
            send_sem=meta_send.at[i], recv_sem=meta_recv.at[me], device_id=taker(i), device_id_type=MESH)

    def in_copy(i):
        return pltpu.make_async_remote_copy(
            src_ref=image_ref.at[:, share(i)], dst_ref=landed.at[slab(me)],
            send_sem=in_send.at[i], recv_sem=in_recv.at[me], device_id=taker(i), device_id_type=MESH)

    def meta_wait(g):
        return pltpu.make_async_copy(meta_ref, meta_all_ref.at[eight(g)], meta_recv.at[g])

    def in_wait(g):
        return pltpu.make_async_copy(image_ref.at[:, share(part)], landed.at[slab(g)], in_recv.at[g])

    def out_copy(g):
        return pltpu.make_async_remote_copy(
            src_ref=final.at[slab(g)], dst_ref=out_ref.at[:, share(part)],
            send_sem=out_send.at[g], recv_sem=out_recv.at[part], device_id=(g, home), device_id_type=MESH)

    def out_wait(i):
        return pltpu.make_async_copy(final.at[slab(me)], out_ref.at[:, share(i)], out_recv.at[i])

    @pl.when(is_home)
    def _():
        meta_wait(me).start()
        in_wait(me).start()

    for make in (meta_copy, in_copy):
        @pl.loop(0, n)
        def _(turn):
            i = lax.rem(turn + me, n)

            @pl.when(jnp.logical_not(jnp.logical_and(is_home, i == part)))
            def _():
                make(i).start()

    @pl.loop(0, n)
    def _(g):
        meta_wait(g).wait()
    to_scalar = pltpu.make_async_copy(meta_all_ref, meta_s, local_sem.at[0])
    to_scalar.start()
    to_scalar.wait()

    def halo_copies(s, group):
        some = slab(group)
        return (
            pltpu.make_async_remote_copy(
                src_ref=send_high.at[s, some], dst_ref=recv_high.at[s, some],
                send_sem=halo_send.at[s, 0, group], recv_sem=halo_recv.at[s, 0, group],
                device_id=next_id, device_id_type=MESH),
            pltpu.make_async_remote_copy(
                src_ref=send_low.at[s, some], dst_ref=recv_low.at[s, some],
                send_sem=halo_send.at[s, 1, group], recv_sem=halo_recv.at[s, 1, group],
                device_id=prev_id, device_id_type=MESH),
        )

    def edges(s, k, b, value):
        send_high[s, k, pl.ds(2 * b, 2), :] = value[rows - 2 : rows]
        send_low[s, k, pl.ds(b, 1), :] = value[0:1]

    @pl.loop(0, n)
    def _(turn):
        group = lax.rem(part - turn + n, n)
        in_wait(group).wait()

        @pl.loop(0, planes, unroll=4)
        def _(inner):
            k = group * planes + inner
            for b in range(blocks):
                value = landed[k, :, pl.ds(b * LANES, LANES)]
                cells_a[k, b, pl.ds(2, rows), :] = value
                edges(0, k, b, value)
        for copy in halo_copies(0, group):
            copy.start()

    tall = cells_a.shape[2]
    lane = lax.broadcasted_iota(jnp.int32, (tall, LANES), 1)
    left = lane >= LANES // 2
    last_two = lane >= LANES - 2
    last_one = lane >= LANES - 1
    first = lane < 1

    for s in range(steps):
        source, target = (cells_a, cells_b) if s % 2 == 0 else (cells_b, cells_a)

        @pl.loop(0, n)
        def _(group):
            for copy in halo_copies(s, group):
                copy.wait_recv()

            @pl.loop(0, planes, unroll=8)
            def _(inner):
                k = group * planes + inner
                for b in range(blocks):
                    source[k, b, pl.ds(0, 2), :] = recv_high[s, k, pl.ds(2 * b, 2), :]
                    source[k, b, pl.ds(rows + 2, 1), :] = recv_low[s, k, pl.ds(b, 1), :]

        def plane(group, inner):
            k = group * planes + inner
            for b in range(blocks):
                spot = (s * planes + inner) * blocks + b
                shift = meta_s[group * 8, spot]
                row = meta_s[group * 8 + 1, spot]
                weight = [table_ref[row, j] for j in range(12)]
                merged = None
                rim = None
                for node in range(4):
                    at = k - shift - 2 + node + 2 * nz
                    at = jnp.bitwise_and(at, nz - 1) if nz & (nz - 1) == 0 else lax.rem(at, nz)
                    own = weight[node] * source[at, b]
                    side = weight[node] * jnp.where(
                        left, source[at, (b - 1) % blocks], source[at, (b + 1) % blocks])
                    merged = own if merged is None else merged + own
                    rim = side if rim is None else rim + side
                along = (
                    weight[8] * pltpu.roll(jnp.where(last_two, rim, merged), 2, 1)
                    + weight[9] * pltpu.roll(jnp.where(last_one, rim, merged), 1, 1)
                    + weight[10] * merged
                    + weight[11] * pltpu.roll(jnp.where(first, rim, merged), LANES - 1, 1)
                )
                value = weight[4] * along[0:rows]
                for node in range(1, 4):
                    value = value + weight[4 + node] * along[node : node + rows]
                if s < steps - 1:
                    target[k, b, pl.ds(2, rows), :] = value
                    edges(s + 1, k, b, value)
                else:
                    final[k, :, pl.ds(b * LANES, LANES)] = value

        if s < steps - 1:
            @pl.loop(0, n)
            def _(group):
                @pl.loop(0, planes, unroll=4)
                def _(inner):
                    plane(group, inner)
                for copy in halo_copies(s + 1, group):
                    copy.start()
        else:
            @pl.loop(0, n)
            def _(turn):
                to = lax.rem(me + turn + 1, n)

                @pl.loop(0, planes, unroll=4)
                def _(inner):
                    plane(to, inner)

                @pl.when(jnp.logical_not(jnp.logical_and(is_home, to == me)))
                def _():
                    out_copy(to).start()

    @pl.when(is_home)
    def _():
        out_wait(part).start()

    @pl.loop(0, n)
    def _(i):
        @pl.when(jnp.logical_not(jnp.logical_and(is_home, i == part)))
        def _():
            meta_copy(i).wait_send()
            in_copy(i).wait_send()

        @pl.when(jnp.logical_not(jnp.logical_and(is_home, i == me)))
        def _():
            out_copy(i).wait_send()

        out_wait(i).wait()

    for s in range(steps):
        @pl.loop(0, n)
        def _(group):
            for copy in halo_copies(s, group):
                copy.wait_send()


def fused(image, offsets, frac_index, fractions, n, n_xy):
    planes, width, depth = image.shape
    steps, blocks = offsets.shape[0], offsets.shape[3]
    rows = width // n
    nz = n * planes
    length = steps * planes * blocks
    padded = -(-length // LANES) * LANES
    meta = jnp.stack([offsets.reshape(length), frac_index.reshape(length)])
    meta = jnp.pad(meta, ((0, 6), (0, padded - length)))
    columns = []
    for axis in range(3):
        columns.extend(cubic_weights(1.0 - fractions[:, axis]))
    table = jnp.stack(columns, axis=1)
    tall = -(-(rows + 3) // 8) * 8
    out, _ = pl.pallas_call(
        functools.partial(fused_kernel, n, n_xy, steps),
        out_shape=(
            jax.ShapeDtypeStruct(image.shape, jnp.float32),
            jax.ShapeDtypeStruct((n * 8, padded), jnp.int32),
        ),
        in_specs=[
            pl.BlockSpec(memory_space=pl.ANY),
            pl.BlockSpec(memory_space=pl.ANY),
            pl.BlockSpec(memory_space=pltpu.SMEM),
        ],
        out_specs=(pl.BlockSpec(memory_space=pl.ANY), pl.BlockSpec(memory_space=pl.ANY)),
        scratch_shapes=[
            pltpu.VMEM((nz, rows, depth), jnp.float32),
            pltpu.VMEM((nz, blocks, tall, LANES), jnp.float32),
            pltpu.VMEM((nz, blocks, tall, LANES), jnp.float32),
            pltpu.VMEM((nz, rows, depth), jnp.float32),
            pltpu.VMEM((steps, nz, 2 * blocks, LANES), jnp.float32),
            pltpu.VMEM((steps, nz, blocks, LANES), jnp.float32),
            pltpu.VMEM((steps, nz, 2 * blocks, LANES), jnp.float32),
            pltpu.VMEM((steps, nz, blocks, LANES), jnp.float32),
            pltpu.SMEM((n * 8, padded), jnp.int32),
            pltpu.SemaphoreType.DMA((n,)),
            pltpu.SemaphoreType.DMA((n,)),
            pltpu.SemaphoreType.DMA((n,)),
            pltpu.SemaphoreType.DMA((n,)),
            pltpu.SemaphoreType.DMA((steps, 2, n)),
            pltpu.SemaphoreType.DMA((steps, 2, n)),
            pltpu.SemaphoreType.DMA((n,)),
            pltpu.SemaphoreType.DMA((n,)),
            pltpu.SemaphoreType.DMA((1,)),
        ],
        compiler_params=pltpu.CompilerParams(
            collective_id=0, has_side_effects=True, vmem_limit_bytes=48 * 1024 * 1024),
    )(image, meta, table)
    return out


def extended(cells, sides, width):
    for axis, dim in sides:
        count = lax.axis_size(axis)
        head = lax.slice_in_dim(cells, 0, width, axis=dim)
        tail = lax.slice_in_dim(cells, cells.shape[dim] - width, cells.shape[dim], axis=dim)
        cells = jnp.concatenate(
            [
                lax.ppermute(tail, axis, [(i, (i + 1) % count) for i in range(count)]),
                cells,
                lax.ppermute(head, axis, [((i + 1) % count, i) for i in range(count)]),
            ],
            axis=dim,
        )
    return cells


def cubic_weights(shares):
    return (
        -shares * (shares - 1.0) * (shares - 2.0) / 6.0,
        (shares + 1.0) * (shares - 1.0) * (shares - 2.0) / 2.0,
        -(shares + 1.0) * shares * (shares - 2.0) / 2.0,
        (shares + 1.0) * shares * (shares - 1.0) / 6.0,
    )


def column_steps(image, offsets, frac_index, fractions):
    step_count = offsets.shape[0]
    all_shifts, all_index = (
        lax.all_gather(offsets, "gz", axis=1, tiled=True),
        lax.all_gather(frac_index, "gz", axis=1, tiled=True),
    )
    standing = jnp.swapaxes(
        lax.all_to_all(image, "gz", split_axis=2, concat_axis=0, tiled=True), 1, 2
    )
    total_planes = standing.shape[0]
    width_y = standing.shape[1]
    width_x = standing.shape[2]
    column_block = lax.axis_index("gz") * width_y // width_x
    block_pick = (jnp.arange(all_shifts.shape[3], dtype=jnp.int32) == column_block).astype(
        jnp.int32
    )
    levels = jnp.arange(total_planes, dtype=jnp.int32)
    table_rows = jnp.arange(fractions.shape[0], dtype=jnp.int32)
    for step_index in range(step_count):
        shifts_now = jnp.sum(all_shifts[step_index, :, 0, :] * block_pick[None, :], axis=1)
        index_now = jnp.sum(all_index[step_index, :, 0, :] * block_pick[None, :], axis=1)
        onehot = (index_now[:, None] == table_rows[None, :]).astype(jnp.float32)
        picked = jnp.dot(onehot, fractions, precision=lax.Precision.HIGHEST)
        zweights = cubic_weights(1.0 - picked[:, 0])
        xweights = cubic_weights(1.0 - picked[:, 1])
        yweights = cubic_weights(1.0 - picked[:, 2])
        rimmed = extended(standing, (("gz", 1), ("xy", 2)), 2)
        merged = jnp.zeros(rimmed.shape, jnp.float32)
        for node in range(4):
            source = jnp.mod(levels - shifts_now - 2 + node, total_planes)
            merged = merged + zweights[node][:, None, None] * jnp.take(rimmed, source, axis=0)
        along_y = jnp.zeros((total_planes, width_y, width_x + 4), jnp.float32)
        for node in range(4):
            along_y = along_y + yweights[node][:, None, None] * merged[:, node : node + width_y, :]
        along_x = jnp.zeros((total_planes, width_y, width_x), jnp.float32)
        for node in range(4):
            along_x = along_x + xweights[node][:, None, None] * along_y[:, :, node : node + width_x]
        standing = along_x
    return lax.all_to_all(
        jnp.swapaxes(standing, 1, 2), "gz", split_axis=0, concat_axis=2, tiled=True
    )


def solution(mesh):
    n, n_xy = mesh.shape["gz"], mesh.shape["xy"]

    def local(image, offsets, frac_index, fractions):
        planes, width, depth = image.shape
        block = depth // offsets.shape[3]
        if block == width == LANES and offsets.shape[2] == 1 and width % (8 * n) == 0 and n > 1:
            return fused(image, offsets, frac_index, fractions, n, n_xy)
        return column_steps(image, offsets, frac_index, fractions)

    in_specs = (P("gz", "xy", None), P(None, "gz", "xy", None), P(None, "gz", "xy", None), P())
    out_specs = P("gz", "xy", None)
    return jax.shard_map(local, mesh=mesh, in_specs=in_specs, out_specs=out_specs, check_vma=False)
```

profile of v0, /device:TPU:15, one launch (start us, length us, event | category | flops | bytes accessed | tf_op | source)
XLA Modules:
  0.0 135.4 jit_solution(5310784741725479753)
XLA Ops:
  0.0 0.8 fusion
  0.8 0.1 copy.25
  0.9 0.1 copy.24
  1.0 0.1 copy.23
  1.0 0.8 copy.15
  1.8 0.1 stack_reshape.6
  1.9 0.8 copy.16
  2.7 0.1 stack_reshape.7
  2.9 0.1 stack.5.table_ref
  3.0 0.0 copy-start
  3.0 1.6 %copy-done = f32[8,128,512]{2,1,0:T(8,128)S(1)} copy-done((f32[8,128,512]{2,1,0:T(8,128)S(1)}, f32[8,128,512]{2,1,0:T(8,128)}, u32[]{:S(2)}) %copy-start) | copy-done | bytes 2097176
  4.6 129.4 %shard_map.46 = (f32[8,128,512]{2,1,0:T(8,128)S(1)}, s32[64,128]{1,0:T(8,128)}) custom-call(f32[8,128,512]{2,1,0:T(8,128)S(1)} %copy-done, s32[8,128]{1,0:T(8,128)S(1)} %pad.4.meta_ref, f32[16,12]{1,0:T(8,128)S(1)} %stack.5.table_ref), custom_call_target="tpu_custom_call" | custom-call | tf_op jit(solution)/shard_map/pallas_call | solution.py:271
  134.0 1.3 copy.27
  (4 shorter events, 0.0 us)
Async XLA Ops:
  3.0 1.6 %copy-start = (f32[8,128,512]{2,1,0:T(8,128)S(1)}, f32[8,128,512]{2,1,0:T(8,128)}, u32[]{:S(2)}) copy-start(f32[8,128,512]{2,1,0:T(8,128)} %image_ref.1) | copy-start | bytes 6291460
where the time goes:
time: 136 us; the launch traced here: 135 us
  Pallas kernels  129 us (95%)
  local copies, waits for them, and re-layouts  5.84 us (4%)
    pallas_call x1, Pallas kernels, fused(): pl.pallas_call(functools.partial(fused_kernel, n, n_xy, steps), out_shape...  129 us
    unnamed x8, local copies, waits for them, and re-layouts  4.74 us

commit v1 on v0

v1 whole, which is shorter than its diff:
```python
import functools

import jax
import jax.numpy as jnp
from jax import lax
from jax.experimental import pallas as pl
from jax.experimental.pallas import tpu as pltpu
from jax.sharding import PartitionSpec as P

MESH = pl.DeviceIdType.MESH
LANES = 128

HALO = 8


def along_path(place, n):
    if n % 2:
        return place
    layer, side = place // 2, place % 2
    return 2 * layer + side + (layer % 2) * (1 - 2 * side)


def slot_of(g, n, strip):
    g = along_path(g, n)
    return g + (strip % 2) * (n - 1 - 2 * g)


def device_at(slot, n, strip):
    return along_path(slot + (strip % 2) * (n - 1 - 2 * slot), n)


def fused_kernel(
    n, n_xy, steps,
    image_ref, meta_ref, fractions_ref, out_ref, meta_all_ref,
    landed, cells_a, cells_b, final, meta_s, shares, table,
    in_send, in_recv, meta_send, meta_recv, alt_sem, alt_recv, halo_send, halo_recv, cross_send,
    out_send, out_recv, local_sem,
):
    planes = image_ref.shape[0]
    width = image_ref.shape[1]
    nz = n * planes
    rows = final.shape[1]
    blocks = final.shape[2] // LANES
    pieces = 2 * n
    mid = n // 2
    me = lax.axis_index("gz")
    xy = lax.axis_index("xy")
    strip, half = xy // 2, lax.rem(xy, 2)
    piece = slot_of(me, n, strip) * 2 + half
    home = strip * 2 + piece // n
    part = lax.rem(piece, n)
    is_home = home == xy
    is_first = part == 0
    is_last = part == n - 1
    cross_up = piece == n - 1
    cross_down = piece == n
    near = (me // mid) * mid

    def holder(line):
        strip_at, piece_at = line // pieces, lax.rem(line, pieces)
        return device_at(piece_at // 2, n, strip_at), strip_at * 2 + lax.rem(piece_at, 2)

    line = strip * pieces + piece
    next_id = holder(lax.rem(line + 1, n * n_xy))
    prev_id = holder(lax.rem(line + n * n_xy - 1, n * n_xy))

    barrier = pltpu.get_barrier_semaphore()
    for i in range(1, pieces):
        other = lax.rem(half * n + me + i, pieces)
        pl.semaphore_signal(
            barrier, inc=1, device_id=(lax.rem(other, n), strip * 2 + other // n), device_id_type=MESH)
    for neighbour in (next_id, prev_id):
        pl.semaphore_signal(barrier, inc=1, device_id=neighbour, device_id_type=MESH)
    pl.semaphore_wait(barrier, pieces + 1)

    def share(i):
        return pl.ds(pl.multiple_of(i * rows, 8), rows)

    def slab(g):
        return pl.ds(g * planes, planes)

    def eight(g):
        return pl.ds(pl.multiple_of(g * 8, 8), 8)

    def taker(i):
        return holder(strip * pieces + half * n + i)

    own_rows = pl.ds(HALO, rows)
    low = -(-steps // 4) * 4
    high_rows, low_rows = pl.ds(0, HALO), pl.ds(HALO + rows, low)

    def meta_copy(i):
        return pltpu.make_async_remote_copy(
            src_ref=meta_ref, dst_ref=meta_all_ref.at[eight(me)],
            send_sem=meta_send.at[i], recv_sem=meta_recv.at[me], device_id=taker(i), device_id_type=MESH)

    def in_copy(i):
        return pltpu.make_async_remote_copy(
            src_ref=image_ref.at[:, share(i)], dst_ref=landed.at[slab(me), own_rows],
            send_sem=in_send.at[i], recv_sem=in_recv.at[me], device_id=taker(i), device_id_type=MESH)

    def meta_wait(g):
        return pltpu.make_async_copy(meta_ref, meta_all_ref.at[eight(g)], meta_recv.at[g])

    def in_wait(g):
        return pltpu.make_async_copy(image_ref.at[:, share(part)], landed.at[slab(g), own_rows], in_recv.at[g])

    def halo_copies(g):
        some = slab(g)
        return (
            (cross_up, pltpu.make_async_remote_copy(
                src_ref=landed.at[some, pl.ds(rows, HALO)], dst_ref=landed.at[some, high_rows],
                send_sem=halo_send.at[0, g], recv_sem=halo_recv.at[0, g],
                device_id=next_id, device_id_type=MESH)),
            (cross_down, pltpu.make_async_remote_copy(
                src_ref=landed.at[some, pl.ds(HALO, low)], dst_ref=landed.at[some, low_rows],
                send_sem=halo_send.at[1, g], recv_sem=halo_recv.at[1, g],
                device_id=prev_id, device_id_type=MESH)),
        )

    def halo_wait(g, side):
        lines = (high_rows, low_rows)[side]
        return pltpu.make_async_copy(
            image_ref.at[:, pl.ds(0, (HALO, low)[side])], landed.at[slab(g), lines], halo_recv.at[side, g])

    cross_id = holder(strip * pieces + n - half)
    cross_own = jnp.logical_and(cross_id[0] == me, cross_id[1] == xy)

    def cross_copies(side):
        lines = (high_rows, low_rows)[side]
        some = image_ref.at[:, pl.ds((width - HALO) * (1 - side), (HALO, low)[side])]
        there = landed.at[slab(me), lines]
        alt = meta_all_ref.at[eight(n + me)]
        return (
            (
                pltpu.make_async_remote_copy(
                    src_ref=meta_ref, dst_ref=alt, send_sem=cross_send.at[1], recv_sem=alt_recv.at[me],
                    device_id=cross_id, device_id_type=MESH),
                pltpu.make_async_remote_copy(
                    src_ref=some, dst_ref=there, send_sem=cross_send.at[0], recv_sem=halo_recv.at[side, me],
                    device_id=cross_id, device_id_type=MESH),
            ),
            (
                pltpu.make_async_copy(meta_ref, alt, alt_recv.at[me]),
                pltpu.make_async_copy(some, there, halo_recv.at[side, me]),
            ),
        )

    def out_copy(g):
        return pltpu.make_async_remote_copy(
            src_ref=final.at[slab(g)], dst_ref=out_ref.at[:, share(part)],
            send_sem=out_send.at[g], recv_sem=out_recv.at[part], device_id=(g, home), device_id_type=MESH)

    def out_wait(i):
        return pltpu.make_async_copy(final.at[slab(me)], out_ref.at[:, share(i)], out_recv.at[i])

    @pl.when(is_home)
    def _():
        meta_wait(me).start()
        in_wait(me).start()

    def send(make, i):
        @pl.when(jnp.logical_not(jnp.logical_and(is_home, i == part)))
        def _():
            make(i).start()

    @pl.loop(0, n)
    def _(turn):
        send(meta_copy, lax.rem(turn + me, n))

    def cross_each(remote, own):
        for side in range(2):
            @pl.when(half == side)
            def _():
                far, here = cross_copies(side)
                if own is not None:
                    @pl.when(cross_own)
                    def _():
                        for copy in here:
                            own(copy)

                @pl.when(jnp.logical_not(cross_own))
                def _():
                    for copy in far:
                        remote(copy)

    cross_each(lambda copy: copy.start(), lambda copy: copy.start())

    @pl.loop(0, mid)
    def _(turn):
        send(in_copy, (1 - half) * mid + lax.rem(turn + me, mid))

    @pl.loop(mid, n)
    def _(turn):
        send(in_copy, half * turn + (1 - half) * (n - 1 - turn))

    get_shares = pltpu.make_async_copy(fractions_ref, shares, local_sem.at[1])
    get_shares.start()
    get_shares.wait()
    for row in range(shares.shape[1]):
        rest = 1.0 - jnp.broadcast_to(shares[:, row : row + 1], (3, LANES))
        for node, weight_of in enumerate(cubic_weights(rest)):
            for axis in range(3):
                table[row, 4 * axis + node] = jnp.broadcast_to(weight_of[axis : axis + 1], (8, LANES))

    @pl.loop(0, n)
    def _(g):
        meta_wait(g).wait()

    own_meta, alt_meta = pl.ds(0, n * 8), pl.ds(n * 8, n * 8)
    outer_first = piece == 0
    outer_last = piece == pieces - 1

    def alt_copy(side):
        return pltpu.make_async_remote_copy(
            src_ref=meta_all_ref.at[own_meta], dst_ref=meta_all_ref.at[alt_meta],
            send_sem=alt_sem.at[0], recv_sem=alt_sem.at[1],
            device_id=(next_id, prev_id)[side], device_id_type=MESH)

    @pl.when(outer_last)
    def _():
        alt_copy(0).start()

    @pl.when(outer_first)
    def _():
        alt_copy(1).start()

    to_scalar = pltpu.make_async_copy(meta_all_ref.at[own_meta], meta_s.at[own_meta], local_sem.at[0])
    to_scalar.start()
    to_scalar.wait()

    @pl.loop(0, n)
    def _(turn):
        g = lax.rem(near + turn, n)
        in_wait(g).wait()
        for left_out, copy in halo_copies(g):
            @pl.when(jnp.logical_not(left_out))
            def _():
                copy.start()

    is_edge = jnp.logical_or(is_first, is_last)

    @pl.when(jnp.logical_or(outer_first, outer_last))
    def _():
        alt_copy(0).wait_recv()

    @pl.when(jnp.logical_or(cross_up, cross_down))
    def _():
        @pl.loop(0, n)
        def _(g):
            pltpu.make_async_copy(meta_ref, meta_all_ref.at[eight(n + g)], alt_recv.at[g]).wait()

    @pl.when(is_edge)
    def _():
        alt_to_scalar = pltpu.make_async_copy(meta_all_ref.at[alt_meta], meta_s.at[alt_meta], local_sem.at[0])
        alt_to_scalar.start()
        alt_to_scalar.wait()

    @pl.loop(0, n)
    def _(g):
        halo_wait(g, 0).wait()
        halo_wait(g, 1).wait()

    lane = lax.broadcasted_iota(jnp.int32, (8, LANES), 1)
    left = lane >= LANES // 2
    last_two = lane >= LANES - 2
    last_one = lane >= LANES - 1
    first = lane < 1

    def weights(base, s, group, inner, b):
        spot = (s * blocks + b) * planes + inner
        shift = meta_s[base + group * 8, spot]
        row = meta_s[base + group * 8 + 1, spot]
        return shift, [table[row, j] for j in range(12)]

    def read(s, at, b, start):
        if s == 0:
            return landed[at, pl.ds(start, 8), pl.ds(b * LANES, LANES)]
        source = cells_a if s % 2 == 1 else cells_b
        return source[at, b, pl.ds(start, 8), :]

    def stencil(s, k, b, shift, weight, start, stop, skip, count):
        spots = []
        for node in range(4):
            at = k - shift - 2 + node + 2 * nz
            spots.append(jnp.bitwise_and(at, nz - 1) if nz & (nz - 1) == 0 else lax.rem(at, nz))
        along = []
        for row in range(start, stop, 8):
            merged = None
            rim = None
            for node, at in enumerate(spots):
                own = weight[node] * read(s, at, b, row)
                side = weight[node] * jnp.where(
                    left, read(s, at, (b - 1) % blocks, row), read(s, at, (b + 1) % blocks, row))
                merged = own if merged is None else merged + own
                rim = side if rim is None else rim + side
            along.append(
                weight[8] * pltpu.roll(jnp.where(last_two, rim, merged), 2, 1)
                + weight[9] * pltpu.roll(jnp.where(last_one, rim, merged), 1, 1)
                + weight[10] * merged
                + weight[11] * pltpu.roll(jnp.where(first, rim, merged), LANES - 1, 1)
            )
        along = jnp.concatenate(along + along[-1:], axis=0)
        parts = []
        for row in range(0, count, 8):
            lines = min(8, along.shape[0] - (skip + row + 3))
            value = weight[4][:lines] * along[skip + row : skip + row + lines]
            for node in range(1, 4):
                value = value + weight[4 + node][:lines] * along[skip + row + node : skip + row + node + lines]
            parts.append(value[: min(lines, count - row)])
        return parts[0] if len(parts) == 1 else jnp.concatenate(parts, axis=0)

    def up(number):
        return -(-number // 8) * 8

    for s in range(steps):
        taken = rows + 3 * (steps - s)
        given = taken - 3
        target = cells_a if s % 2 == 0 else cells_b

        def plane(group, inner):
            k = group * planes + inner
            for b in range(blocks):
                shift, weight = weights(0, s, group, inner, b)
                value = stencil(s, k, b, shift, weight, 0, up(taken), 0, given)
                if s < steps - 1:
                    target[k, b, pl.ds(0, given), :] = value
                else:
                    final[k, :, pl.ds(b * LANES, LANES)] = value

        if s < steps - 1:
            @pl.loop(0, n)
            def _(group):
                @pl.loop(0, planes, unroll=4)
                def _(inner):
                    plane(group, inner)

            ahead = 2 * (steps - 1 - s)
            edge = rows + ahead
            for flag, start, stop, skip, row, count in (
                (is_first, 0, up(ahead + 3), 0, 0, ahead),
                (is_last, edge // 8 * 8, up(taken), edge % 8, edge, given - edge),
            ):
                @pl.when(flag)
                def _():
                    @pl.loop(0, n)
                    def _(group):
                        @pl.loop(0, planes, unroll=8)
                        def _(inner):
                            k = group * planes + inner
                            for b in range(blocks):
                                shift, weight = weights(n * 8, s, group, inner, b)
                                target[k, b, pl.ds(row, count), :] = stencil(
                                    s, k, b, shift, weight, start, stop, skip, count)
        else:
            for far in (1, 0):
                @pl.loop(0, mid)
                def _(turn):
                    to = lax.rem(near + far * mid, n) + lax.rem(turn + me, mid)

                    @pl.loop(0, planes, unroll=4)
                    def _(inner):
                        plane(to, inner)

                    @pl.when(jnp.logical_not(jnp.logical_and(is_home, to == me)))
                    def _():
                        out_copy(to).start()

    @pl.when(is_home)
    def _():
        out_wait(part).start()

    @pl.loop(0, n)
    def _(i):
        @pl.when(jnp.logical_not(jnp.logical_and(is_home, i == part)))
        def _():
            meta_copy(i).wait_send()
            in_copy(i).wait_send()

        for left_out, copy in halo_copies(i):
            @pl.when(jnp.logical_not(left_out))
            def _():
                copy.wait_send()

        @pl.when(jnp.logical_not(jnp.logical_and(is_home, i == me)))
        def _():
            out_copy(i).wait_send()

        out_wait(i).wait()

    cross_each(lambda copy: copy.wait_send(), None)

    @pl.when(jnp.logical_or(outer_first, outer_last))
    def _():
        alt_copy(0).wait_send()


def fused(image, offsets, frac_index, fractions, n, n_xy):
    planes, width, depth = image.shape
    steps, blocks = offsets.shape[0], offsets.shape[3]
    rows = width // n
    nz = n * planes
    length = steps * planes * blocks
    padded = -(-length // LANES) * LANES
    meta = jnp.transpose(jnp.stack([offsets, frac_index]), (0, 1, 3, 4, 2)).reshape(2, length)
    meta = jnp.pad(meta, ((0, 6), (0, padded - length)))
    table = fractions.T
    tall = -(-(rows + 3 * steps) // 8) * 8
    out, _ = pl.pallas_call(
        functools.partial(fused_kernel, n, n_xy, steps),
        out_shape=(
            jax.ShapeDtypeStruct(image.shape, jnp.float32),
            jax.ShapeDtypeStruct((2 * n * 8, padded), jnp.int32),
        ),
        in_specs=[
            pl.BlockSpec(memory_space=pl.ANY),
            pl.BlockSpec(memory_space=pl.ANY),
            pl.BlockSpec(memory_space=pl.ANY),
        ],
        out_specs=(pl.BlockSpec(memory_space=pl.ANY), pl.BlockSpec(memory_space=pl.ANY)),
        scratch_shapes=[
            pltpu.VMEM((nz, rows + 2 * HALO, depth), jnp.float32),
            pltpu.VMEM((nz, blocks, tall, LANES), jnp.float32),
            pltpu.VMEM((nz, blocks, tall, LANES), jnp.float32),
            pltpu.VMEM((nz, rows, depth), jnp.float32),
            pltpu.SMEM((2 * n * 8, padded), jnp.int32),
            pltpu.VMEM(table.shape, jnp.float32),
            pltpu.VMEM((table.shape[1], 12, 8, LANES), jnp.float32),
            pltpu.SemaphoreType.DMA((n,)),
            pltpu.SemaphoreType.DMA((n,)),
            pltpu.SemaphoreType.DMA((n,)),
            pltpu.SemaphoreType.DMA((n,)),
            pltpu.SemaphoreType.DMA((2,)),
            pltpu.SemaphoreType.DMA((n,)),
            pltpu.SemaphoreType.DMA((2, n)),
            pltpu.SemaphoreType.DMA((2, n)),
            pltpu.SemaphoreType.DMA((2,)),
            pltpu.SemaphoreType.DMA((n,)),
            pltpu.SemaphoreType.DMA((n,)),
            pltpu.SemaphoreType.DMA((2,)),
        ],
        compiler_params=pltpu.CompilerParams(
            collective_id=0, has_side_effects=True, vmem_limit_bytes=48 * 1024 * 1024),
    )(image, meta, table)
    return out


def extended(cells, sides, width):
    for axis, dim in sides:
        count = lax.axis_size(axis)
        head = lax.slice_in_dim(cells, 0, width, axis=dim)
        tail = lax.slice_in_dim(cells, cells.shape[dim] - width, cells.shape[dim], axis=dim)
        cells = jnp.concatenate(
            [
                lax.ppermute(tail, axis, [(i, (i + 1) % count) for i in range(count)]),
                cells,
                lax.ppermute(head, axis, [((i + 1) % count, i) for i in range(count)]),
            ],
            axis=dim,
        )
    return cells


def cubic_weights(shares):
    return (
        -shares * (shares - 1.0) * (shares - 2.0) / 6.0,
        (shares + 1.0) * (shares - 1.0) * (shares - 2.0) / 2.0,
        -(shares + 1.0) * shares * (shares - 2.0) / 2.0,
        (shares + 1.0) * shares * (shares - 1.0) / 6.0,
    )


def column_steps(image, offsets, frac_index, fractions):
    step_count = offsets.shape[0]
    all_shifts, all_index = (
        lax.all_gather(offsets, "gz", axis=1, tiled=True),
        lax.all_gather(frac_index, "gz", axis=1, tiled=True),
    )
    standing = jnp.swapaxes(
        lax.all_to_all(image, "gz", split_axis=2, concat_axis=0, tiled=True), 1, 2
    )
    total_planes = standing.shape[0]
    width_y = standing.shape[1]
    width_x = standing.shape[2]
    column_block = lax.axis_index("gz") * width_y // width_x
    block_pick = (jnp.arange(all_shifts.shape[3], dtype=jnp.int32) == column_block).astype(
        jnp.int32
    )
    levels = jnp.arange(total_planes, dtype=jnp.int32)
    table_rows = jnp.arange(fractions.shape[0], dtype=jnp.int32)
    for step_index in range(step_count):
        shifts_now = jnp.sum(all_shifts[step_index, :, 0, :] * block_pick[None, :], axis=1)
        index_now = jnp.sum(all_index[step_index, :, 0, :] * block_pick[None, :], axis=1)
        onehot = (index_now[:, None] == table_rows[None, :]).astype(jnp.float32)
        picked = jnp.dot(onehot, fractions, precision=lax.Precision.HIGHEST)
        zweights = cubic_weights(1.0 - picked[:, 0])
        xweights = cubic_weights(1.0 - picked[:, 1])
        yweights = cubic_weights(1.0 - picked[:, 2])
        rimmed = extended(standing, (("gz", 1), ("xy", 2)), 2)
        merged = jnp.zeros(rimmed.shape, jnp.float32)
        for node in range(4):
            source = jnp.mod(levels - shifts_now - 2 + node, total_planes)
            merged = merged + zweights[node][:, None, None] * jnp.take(rimmed, source, axis=0)
        along_y = jnp.zeros((total_planes, width_y, width_x + 4), jnp.float32)
        for node in range(4):
            along_y = along_y + yweights[node][:, None, None] * merged[:, node : node + width_y, :]
        along_x = jnp.zeros((total_planes, width_y, width_x), jnp.float32)
        for node in range(4):
            along_x = along_x + xweights[node][:, None, None] * along_y[:, :, node : node + width_x]
        standing = along_x
    return lax.all_to_all(
        jnp.swapaxes(standing, 1, 2), "gz", split_axis=0, concat_axis=2, tiled=True
    )


def solution(mesh):
    n, n_xy = mesh.shape["gz"], mesh.shape["xy"]

    def local(image, offsets, frac_index, fractions):
        planes, width, depth = image.shape
        block = depth // offsets.shape[3]
        if block == width == LANES and offsets.shape[2] == 1 and width % (8 * n) == 0 and n % 2 == 0 and n_xy % 2 == 0 and 2 * offsets.shape[0] <= HALO:
            return fused(image, offsets, frac_index, fractions, n, n_xy)
        return column_steps(image, offsets, frac_index, fractions)

    in_specs = (P("gz", "xy", None), P(None, "gz", "xy", None), P(None, "gz", "xy", None), P())
    out_specs = P("gz", "xy", None)
    return jax.shard_map(local, mesh=mesh, in_specs=in_specs, out_specs=out_specs, check_vma=False)
```

time: 136 us -> 123 us (0.904)
  Pallas kernels: 129 us -> 118 us
  local copies, waits for them, and re-layouts: 5.84 us -> 3.69 us
    pallas_call x1, Pallas kernels: 129 us -> 118 us  [fused(): pl.pallas_call(functools.partial(fused_kernel, n, n_xy, steps), out_shape...]
    unnamed x8 -> x5, local copies, waits for them, and re-layouts: 4.74 us -> 3.59 us
where the time goes in v1:
time: 123 us; the launch traced here: 122 us
  Pallas kernels  118 us (96%)
  local copies, waits for them, and re-layouts  3.69 us (3%)
    pallas_call x1, Pallas kernels, fused(): pl.pallas_call(functools.partial(fused_kernel, n, n_xy, steps), out_shape...  118 us
    unnamed x5, local copies, waits for them, and re-layouts  3.59 us

profile of v1, /device:TPU:15, one launch (start us, length us, event | category | flops | bytes accessed | tf_op | source)
XLA Modules:
  0.0 122.3 jit_solution(11845161277033062864)
XLA Ops:
  0.0 0.7 add_bitcast_fusion
  0.7 0.1 reshape.3
  0.8 0.0 copy-start
  0.8 1.6 %copy-done = f32[8,128,512]{2,1,0:T(8,128)S(1)} copy-done((f32[8,128,512]{2,1,0:T(8,128)S(1)}, f32[8,128,512]{2,1,0:T(8,128)}, u32[]{:S(2)}) %copy-start) | copy-done | bytes 2097176
  2.4 0.0 copy-start.1
  2.4 0.7 copy-done.1
  3.1 117.9 %shard_map.46 = (f32[8,128,512]{2,1,0:T(8,128)S(1)}, s32[128,128]{1,0:T(8,128)}) custom-call(f32[8,128,512]{2,1,0:T(8,128)S(1)} %copy-done, s32[8,128]{1,0:T(8,128)S(1)} %pad.4.meta_ref, f32[3,16]{1,0:T(4,128)S(1)} %bitcast.7), custom_call_target="tpu_custom_call" | custom-call | tf_op jit(solution)/shard_map/pallas_call | solution.py:409
  121.0 1.3 %copy.6 = f32[8,128,512]{2,1,0:T(8,128)} copy(f32[8,128,512]{2,1,0:T(8,128)S(1)} %get-tuple-element.6) | data formatting | bytes 4194304
  (1 shorter events, 0.0 us)
Async XLA Ops:
  0.8 1.6 %copy-start = (f32[8,128,512]{2,1,0:T(8,128)S(1)}, f32[8,128,512]{2,1,0:T(8,128)}, u32[]{:S(2)}) copy-start(f32[8,128,512]{2,1,0:T(8,128)} %image_ref.1) | copy-start | bytes 6291460
  2.4 0.7 copy-start.1

commit v2 on v1

--- a/solution.py
+++ b/solution.py
@@ -20,19 +20,30 @@
     return 2 * layer + side + (layer % 2) * (1 - 2 * side)
 
 
-def slot_of(g, n, strip):
-    g = along_path(g, n)
-    return g + (strip % 2) * (n - 1 - 2 * g)
-
-
-def device_at(slot, n, strip):
-    return along_path(slot + (strip % 2) * (n - 1 - 2 * slot), n)
+def piece_of(g, core, n, pair):
+    mid = n // 2
+    slot = along_path(g, n)
+    right = slot // mid
+    place = slot + right * (n - 1 - 2 * slot)
+    piece = core * (mid + place) + (1 - core) * (mid - 1 - place)
+    flip = lax.rem(right + pair, 2)
+    return piece + flip * (2 * n - 1 - 2 * piece)
+
+
+def device_at(piece, n, pair):
+    mid = n // 2
+    piece = piece + lax.rem(pair, 2) * (2 * n - 1 - 2 * piece)
+    right = piece // n
+    piece = piece + right * (2 * n - 1 - 2 * piece)
+    core = piece // mid
+    place = core * (piece - mid) + (1 - core) * (mid - 1 - piece)
+    return along_path(place + right * (n - 1 - 2 * place), n), pair * 2 + core
 
 
 def fused_kernel(
     n, n_xy, steps,
     image_ref, meta_ref, fractions_ref, out_ref, meta_all_ref,
-    landed, cells_a, cells_b, final, meta_s, shares, table,
+    landed, high, low, cells_a, cells_b, sides_a, sides_b, final, meta_s, shares, table,
     in_send, in_recv, meta_send, meta_recv, alt_sem, alt_recv, halo_send, halo_recv, cross_send,
     out_send, out_recv, local_sem,
 ):
@@ -46,7 +57,7 @@
     me = lax.axis_index("gz")
     xy = lax.axis_index("xy")
     strip, half = xy // 2, lax.rem(xy, 2)
-    piece = slot_of(me, n, strip) * 2 + half
+    piece = piece_of(me, half, n, strip)
     home = strip * 2 + piece // n
     part = lax.rem(piece, n)
     is_home = home == xy
@@ -57,8 +68,7 @@
     near = (me // mid) * mid
 
     def holder(line):
-        strip_at, piece_at = line // pieces, lax.rem(line, pieces)
-        return device_at(piece_at // 2, n, strip_at), strip_at * 2 + lax.rem(piece_at, 2)
+        return device_at(lax.rem(line, pieces), n, line // pieces)
 
     line = strip * pieces + piece
     next_id = holder(lax.rem(line + 1, n * n_xy))
@@ -85,9 +95,8 @@
     def taker(i):
         return holder(strip * pieces + half * n + i)
 
-    own_rows = pl.ds(HALO, rows)
-    low = -(-steps // 4) * 4
-    high_rows, low_rows = pl.ds(0, HALO), pl.ds(HALO + rows, low)
+    beside = (high, low)
+    deep = low.shape[1]
 
     def meta_copy(i):
         return pltpu.make_async_remote_copy(
@@ -96,40 +105,38 @@
 
     def in_copy(i):
         return pltpu.make_async_remote_copy(
-            src_ref=image_ref.at[:, share(i)], dst_ref=landed.at[slab(me), own_rows],
+            src_ref=image_ref.at[:, share(i)], dst_ref=landed.at[slab(me)],
             send_sem=in_send.at[i], recv_sem=in_recv.at[me], device_id=taker(i), device_id_type=MESH)
 
     def meta_wait(g):
         return pltpu.make_async_copy(meta_ref, meta_all_ref.at[eight(g)], meta_recv.at[g])
 
     def in_wait(g):
-        return pltpu.make_async_copy(image_ref.at[:, share(part)], landed.at[slab(g), own_rows], in_recv.at[g])
+        return pltpu.make_async_copy(image_ref.at[:, share(part)], landed.at[slab(g)], in_recv.at[g])
 
     def halo_copies(g):
         some = slab(g)
         return (
             (cross_up, pltpu.make_async_remote_copy(
-                src_ref=landed.at[some, pl.ds(rows, HALO)], dst_ref=landed.at[some, high_rows],
+                src_ref=landed.at[some, pl.ds(rows - HALO, HALO)], dst_ref=high.at[some],
                 send_sem=halo_send.at[0, g], recv_sem=halo_recv.at[0, g],
                 device_id=next_id, device_id_type=MESH)),
             (cross_down, pltpu.make_async_remote_copy(
-                src_ref=landed.at[some, pl.ds(HALO, low)], dst_ref=landed.at[some, low_rows],
+                src_ref=landed.at[some, pl.ds(0, deep)], dst_ref=low.at[some],
                 send_sem=halo_send.at[1, g], recv_sem=halo_recv.at[1, g],
                 device_id=prev_id, device_id_type=MESH)),
         )
 
     def halo_wait(g, side):
-        lines = (high_rows, low_rows)[side]
         return pltpu.make_async_copy(
-            image_ref.at[:, pl.ds(0, (HALO, low)[side])], landed.at[slab(g), lines], halo_recv.at[side, g])
+            image_ref.at[:, pl.ds(0, (HALO, deep)[side])], beside[side].at[slab(g)], halo_recv.at[side, g])
 
     cross_id = holder(strip * pieces + n - half)
     cross_own = jnp.logical_and(cross_id[0] == me, cross_id[1] == xy)
 
     def cross_copies(side):
-        lines = (high_rows, low_rows)[side]
-        some = image_ref.at[:, pl.ds((width - HALO) * (1 - side), (HALO, low)[side])]
-        there = landed.at[slab(me), lines]
+        some = image_ref.at[:, pl.ds((width - HALO) * (1 - side), (HALO, deep)[side])]
+        there = beside[side].at[slab(me)]
         alt = meta_all_ref.at[eight(n + me)]
         return (
             (
@@ -190,9 +197,13 @@
     def _(turn):
         send(in_copy, (1 - half) * mid + lax.rem(turn + me, mid))
 
+    in_middle = jnp.logical_and(piece >= mid, piece < pieces - mid)
+
     @pl.loop(mid, n)
     def _(turn):
-        send(in_copy, half * turn + (1 - half) * (n - 1 - turn))
+        @pl.when(jnp.logical_not(in_middle))
+        def _():
+            send(in_copy, half * turn + (1 - half) * (n - 1 - turn))
 
     get_shares = pltpu.make_async_copy(fractions_ref, shares, local_sem.at[1])
     get_shares.start()
@@ -238,6 +249,11 @@
             def _():
                 copy.start()
 
+        @pl.when(jnp.logical_and(in_middle, lax.rem(turn, 2) == 0))
+        def _():
+            later = mid + turn // 2
+            send(in_copy, half * later + (1 - half) * (n - 1 - later))
+
     is_edge = jnp.logical_or(is_first, is_last)
 
     @pl.when(jnp.logical_or(outer_first, outer_last))
@@ -255,11 +271,6 @@
         alt_to_scalar = pltpu.make_async_copy(meta_all_ref.at[alt_meta], meta_s.at[alt_meta], local_sem.at[0])
         alt_to_scalar.start()
         alt_to_scalar.wait()
-
-    @pl.loop(0, n)
-    def _(g):
-        halo_wait(g, 0).wait()
-        halo_wait(g, 1).wait()
 
     lane = lax.broadcasted_iota(jnp.int32, (8, LANES), 1)
     left = lane >= LANES // 2
@@ -273,34 +284,52 @@
         row = meta_s[base + group * 8 + 1, spot]
         return shift, [table[row, j] for j in range(12)]
 
-    def read(s, at, b, start):
-        if s == 0:
-            return landed[at, pl.ds(start, 8), pl.ds(b * LANES, LANES)]
-        source = cells_a if s % 2 == 1 else cells_b
-        return source[at, b, pl.ds(start, 8), :]
-
-    def stencil(s, k, b, shift, weight, start, stop, skip, count):
+    cells, sides = (cells_b, cells_a), (sides_b, sides_a)
+
+    def read(s, at, b, row):
+        if s > 0:
+            return cells[s % 2][at, b, pl.ds(row, 8), :]
+        lanes = pl.ds(b * LANES, LANES)
+        if row < HALO:
+            return high[at, :, lanes]
+        if row < HALO + rows:
+            return landed[at, pl.ds(row - HALO, 8), lanes]
+        return low[at, :, lanes]
+
+    def beyond(s, at, b, row):
+        if s > 0:
+            return sides[s % 2][at, b, pl.ds(row, 8), :]
+        before = read(s, at, (b - 1) % blocks, row)
+        return jnp.where(left[: before.shape[0]], before, read(s, at, (b + 1) % blocks, row))
+
+    def across(s, k, b, shift, weight, start, stop):
         spots = []
         for node in range(4):
             at = k - shift - 2 + node + 2 * nz
             spots.append(jnp.bitwise_and(at, nz - 1) if nz & (nz - 1) == 0 else lax.rem(at, nz))
         along = []
         for row in range(start, stop, 8):
+            lines = deep if s == 0 and row >= HALO + rows else 8
+            own_weight = [w[:lines] for w in weight]
             merged = None
             rim = None
             for node, at in enumerate(spots):
-                own = weight[node] * read(s, at, b, row)
-                side = weight[node] * jnp.where(
-                    left, read(s, at, (b - 1) % blocks, row), read(s, at, (b + 1) % blocks, row))
+                own = own_weight[node] * read(s, at, b, row)
+                side = own_weight[node] * beyond(s, at, b, row)
                 merged = own if merged is None else merged + own
                 rim = side if rim is None else rim + side
             along.append(
-                weight[8] * pltpu.roll(jnp.where(last_two, rim, merged), 2, 1)
-                + weight[9] * pltpu.roll(jnp.where(last_one, rim, merged), 1, 1)
-                + weight[10] * merged
-                + weight[11] * pltpu.roll(jnp.where(first, rim, merged), LANES - 1, 1)
+                own_weight[8] * pltpu.roll(jnp.where(last_two[:lines], rim, merged), 2, 1)
+                + own_weight[9] * pltpu.roll(jnp.where(last_one[:lines], rim, merged), 1, 1)
+                + own_weight[10] * merged
+                + own_weight[11] * pltpu.roll(jnp.where(first[:lines], rim, merged), LANES - 1, 1)
             )
-        along = jnp.concatenate(along + along[-1:], axis=0)
+        return along
+
+    def down(weight, along, skip, count):
+        if along[-1].shape[0] == 8:
+            along = along + along[-1:]
+        along = jnp.concatenate(along, axis=0)
         parts = []
         for row in range(0, count, 8):
             lines = min(8, along.shape[0] - (skip + row + 3))
@@ -310,30 +339,60 @@
             parts.append(value[: min(lines, count - row)])
         return parts[0] if len(parts) == 1 else jnp.concatenate(parts, axis=0)
 
+    def keep(s, k, row, values):
+        count = values[0].shape[0]
+        mine = lax.broadcasted_iota(jnp.int32, (count, LANES), 1) >= LANES // 2
+        for b in range(blocks):
+            there = pl.ds(row, count)
+            cells[(s + 1) % 2][k, b, there, :] = values[b]
+            sides[(s + 1) % 2][k, b, there, :] = jnp.where(
+                mine, values[(b - 1) % blocks], values[(b + 1) % blocks])
+
+    def each_plane(unroll, body):
+        @pl.loop(0, n)
+        def _(group):
+            @pl.loop(0, planes, unroll=unroll)
+            def _(inner):
+                body(group, inner)
+
     def up(number):
         return -(-number // 8) * 8
+
+    def inside(group, inner):
+        k = group * planes + inner
+        for b in range(blocks):
+            shift, weight = weights(0, 0, group, inner, b)
+            along = across(0, k, b, shift, weight, HALO, HALO + rows)
+            for i, lines in enumerate(along):
+                cells_b[k, b, pl.ds(HALO + 8 * i, 8), :] = lines
+
+    each_plane(8, inside)
+
+    @pl.loop(0, n)
+    def _(g):
+        halo_wait(g, 0).wait()
+        halo_wait(g, 1).wait()
 
     for s in range(steps):
         taken = rows + 3 * (steps - s)
         given = taken - 3
-        target = cells_a if s % 2 == 0 else cells_b
-
-        def plane(group, inner):
+
+        def values_of(group, inner):
             k = group * planes + inner
+            values = []
             for b in range(blocks):
                 shift, weight = weights(0, s, group, inner, b)
-                value = stencil(s, k, b, shift, weight, 0, up(taken), 0, given)
-                if s < steps - 1:
-                    target[k, b, pl.ds(0, given), :] = value
+                if s == 0:
+                    along = across(s, k, b, shift, weight, 0, HALO)
+                    along += [cells_b[k, b, pl.ds(row, 8), :] for row in range(HALO, HALO + rows, 8)]
+                    along += across(s, k, b, shift, weight, HALO + rows, up(taken))
                 else:
-                    final[k, :, pl.ds(b * LANES, LANES)] = value
+                    along = across(s, k, b, shift, weight, 0, up(taken))
+                values.append(down(weight, along, 0, given))
+            return values
 
         if s < steps - 1:
-            @pl.loop(0, n)
-            def _(group):
-                @pl.loop(0, planes, unroll=4)
-                def _(inner):
-                    plane(group, inner)
+            each_plane(8, lambda group, inner: keep(s, group * planes + inner, 0, values_of(group, inner)))
 
             ahead = 2 * (steps - 1 - s)
             edge = rows + ahead
@@ -343,24 +402,25 @@
             ):
                 @pl.when(flag)
                 def _():
-                    @pl.loop(0, n)
-                    def _(group):
-                        @pl.loop(0, planes, unroll=8)
-                        def _(inner):
-                            k = group * planes + inner
-                            for b in range(blocks):
-                                shift, weight = weights(n * 8, s, group, inner, b)
-                                target[k, b, pl.ds(row, count), :] = stencil(
-                                    s, k, b, shift, weight, start, stop, skip, count)
+                    def beside_plane(group, inner):
+                        values = []
+                        for b in range(blocks):
+                            shift, weight = weights(n * 8, s, group, inner, b)
+                            along = across(s, group * planes + inner, b, shift, weight, start, stop)
+                            values.append(down(weight, along, skip, count))
+                        keep(s, group * planes + inner, row, values)
+
+                    each_plane(8, beside_plane)
         else:
             for far in (1, 0):
                 @pl.loop(0, mid)
                 def _(turn):
                     to = lax.rem(near + far * mid, n) + lax.rem(turn + me, mid)
 
-                    @pl.loop(0, planes, unroll=4)
+                    @pl.loop(0, planes, unroll=8)
                     def _(inner):
-                        plane(to, inner)
+                        for b, value in enumerate(values_of(to, inner)):
+                            final[to * planes + inner, :, pl.ds(b * LANES, LANES)] = value
 
                     @pl.when(jnp.logical_not(jnp.logical_and(is_home, to == me)))
                     def _():
@@ -419,7 +479,11 @@
         ],
         out_specs=(pl.BlockSpec(memory_space=pl.ANY), pl.BlockSpec(memory_space=pl.ANY)),
         scratch_shapes=[
-            pltpu.VMEM((nz, rows + 2 * HALO, depth), jnp.float32),
+            pltpu.VMEM((nz, rows, depth), jnp.float32),
+            pltpu.VMEM((nz, HALO, depth), jnp.float32),
+            pltpu.VMEM((nz, -(-steps // 4) * 4, depth), jnp.float32),
+            pltpu.VMEM((nz, blocks, tall, LANES), jnp.float32),
+            pltpu.VMEM((nz, blocks, tall, LANES), jnp.float32),
             pltpu.VMEM((nz, blocks, tall, LANES), jnp.float32),
             pltpu.VMEM((nz, blocks, tall, LANES), jnp.float32),
             pltpu.VMEM((nz, rows, depth), jnp.float32),

time: 123 us -> 117 us (0.951)
  Pallas kernels: 118 us -> 111 us
    pallas_call x1, Pallas kernels: 118 us -> 111 us  [fused(): pl.pallas_call(functools.partial(fused_kernel, n, n_xy, steps), out_shape...]
where the time goes in v2:
time: 117 us; the launch traced here: 116 us
  Pallas kernels  111 us (95%)
  local copies, waits for them, and re-layouts  3.69 us (3%)
    pallas_call x1, Pallas kernels, fused(): pl.pallas_call(functools.partial(fused_kernel, n, n_xy, steps), out_shape...  111 us
    unnamed x5, local copies, waits for them, and re-layouts  3.59 us

profile of v2, /device:TPU:15, one launch (start us, length us, event | category | flops | bytes accessed | tf_op | source)
XLA Modules:
  0.0 115.8 jit_solution(1370127667269983367)
XLA Ops:
  0.0 0.7 add_bitcast_fusion
  0.7 0.1 reshape.3
  0.8 0.0 copy-start
  0.8 1.6 %copy-done = f32[8,128,512]{2,1,0:T(8,128)S(1)} copy-done((f32[8,128,512]{2,1,0:T(8,128)S(1)}, f32[8,128,512]{2,1,0:T(8,128)}, u32[]{:S(2)}) %copy-start) | copy-done | bytes 2097176
  2.4 0.0 copy-start.1
  2.4 0.7 copy-done.1
  3.1 111.4 %shard_map.46 = (f32[8,128,512]{2,1,0:T(8,128)S(1)}, s32[128,128]{1,0:T(8,128)}) custom-call(f32[8,128,512]{2,1,0:T(8,128)S(1)} %copy-done, s32[8,128]{1,0:T(8,128)S(1)} %pad.4.meta_ref, f32[3,16]{1,0:T(4,128)S(1)} %bitcast.7), custom_call_target="tpu_custom_call" | custom-call | tf_op jit(solution)/shard_map/pallas_call | solution.py:469
  114.5 1.3 %copy.6 = f32[8,128,512]{2,1,0:T(8,128)} copy(f32[8,128,512]{2,1,0:T(8,128)S(1)} %get-tuple-element.6) | data formatting | bytes 4194304
  (1 shorter events, 0.0 us)
Async XLA Ops:
  0.8 1.6 %copy-start = (f32[8,128,512]{2,1,0:T(8,128)S(1)}, f32[8,128,512]{2,1,0:T(8,128)}, u32[]{:S(2)}) copy-start(f32[8,128,512]{2,1,0:T(8,128)} %image_ref.1) | copy-start | bytes 6291460
  2.4 0.7 copy-start.1

commit v3 on v2

--- a/solution.py
+++ b/solution.py
@@ -191,11 +191,11 @@
                     for copy in far:
                         remote(copy)
 
-    cross_each(lambda copy: copy.start(), lambda copy: copy.start())
-
     @pl.loop(0, mid)
     def _(turn):
         send(in_copy, (1 - half) * mid + lax.rem(turn + me, mid))
+
+    cross_each(lambda copy: copy.start(), lambda copy: copy.start())
 
     in_middle = jnp.logical_and(piece >= mid, piece < pieces - mid)
 
@@ -415,7 +415,7 @@
             for far in (1, 0):
                 @pl.loop(0, mid)
                 def _(turn):
-                    to = lax.rem(near + far * mid, n) + lax.rem(turn + me, mid)
+                    to = lax.rem(near + far * mid, n) + lax.rem(turn + me + 2 * half, mid)
 
                     @pl.loop(0, planes, unroll=8)
                     def _(inner):

time: 117 us -> 117 us (level)
  no operation moved by 1% of the time
where the time goes in v3:
time: 117 us; the launch traced here: 115 us
  Pallas kernels  111 us (95%)
  local copies, waits for them, and re-layouts  3.69 us (3%)
    pallas_call x1, Pallas kernels, fused(): pl.pallas_call(functools.partial(fused_kernel, n, n_xy, steps), out_shape...  111 us
    unnamed x5, local copies, waits for them, and re-layouts  3.59 us

profile of v3, /device:TPU:15, one launch (start us, length us, event | category | flops | bytes accessed | tf_op | source)
XLA Modules:
  0.0 115.4 jit_solution(6992634071394032645)
XLA Ops:
  0.0 0.7 add_bitcast_fusion
  0.7 0.1 reshape.3
  0.8 0.0 copy-start
  0.8 1.6 %copy-done = f32[8,128,512]{2,1,0:T(8,128)S(1)} copy-done((f32[8,128,512]{2,1,0:T(8,128)S(1)}, f32[8,128,512]{2,1,0:T(8,128)}, u32[]{:S(2)}) %copy-start) | copy-done | bytes 2097176
  2.4 0.0 copy-start.1
  2.4 0.7 copy-done.1
  3.1 111.0 %shard_map.46 = (f32[8,128,512]{2,1,0:T(8,128)S(1)}, s32[128,128]{1,0:T(8,128)}) custom-call(f32[8,128,512]{2,1,0:T(8,128)S(1)} %copy-done, s32[8,128]{1,0:T(8,128)S(1)} %pad.4.meta_ref, f32[3,16]{1,0:T(4,128)S(1)} %bitcast.7), custom_call_target="tpu_custom_call" | custom-call | tf_op jit(solution)/shard_map/pallas_call | solution.py:469
  114.1 1.3 %copy.6 = f32[8,128,512]{2,1,0:T(8,128)} copy(f32[8,128,512]{2,1,0:T(8,128)S(1)} %get-tuple-element.6) | data formatting | bytes 4194304
  (1 shorter events, 0.0 us)
Async XLA Ops:
  0.8 1.6 %copy-start = (f32[8,128,512]{2,1,0:T(8,128)S(1)}, f32[8,128,512]{2,1,0:T(8,128)}, u32[]{:S(2)}) copy-start(f32[8,128,512]{2,1,0:T(8,128)} %image_ref.1) | copy-start | bytes 6291460
  2.4 0.7 copy-start.1
